TPU v7x, 128 devices: a whole 4x4x4 slice. The times are simulated.
128 devices in a mesh: wide: 32 (over y, z, core), narrow: 4 (over x).
Axes of the slice: x: 4, y: 4, z: 4, core: 2. Of those that a mesh axis runs over, the one named last changes fastest.
Arguments:
- object_field: float32 [2, 2048, 16384], P(None, 'narrow', 'wide')
- probe: float32 [4, 2, 256, 256], replicated, may hold values from -3 to 3
- patterns: float32 [4, 32, 6, 256, 256], P('narrow', 'wide'), may hold values from 0.1 to 4
- offsets: int32 [4, 32, 6, 2], P('narrow', 'wide'), may hold values from -128 to 384
- counts: int32 [4, 32], P('narrow', 'wide'), may hold values from 1 to 6
Outputs:
- object_new: float32 [2, 2048, 16384], P(None, 'narrow', 'wide')
- probe_new: float32 [4, 2, 256, 256], replicated
Inputs may be any that keep to these rules, and one draw needn't show every extreme that they name: A patch of 256 x 256 pixels at these offsets stays within the tile extended by 128 pixels on each side. `counts`: slots 0 to count - 1 of a tile are live, the others are ignored.
All inputs are finite; a program needn't handle non-finite values.
Results may differ from a plain program's by a relative error of at most 0.0003.
Values sent between devices are 32-bit elements; how exact they have to be, the bound alone decides.
A program may use at most 128 MiB of HBM per device.

v0:
```python
import jax
import jax.numpy as jnp
from jax import lax
from jax.sharding import PartitionSpec as P

H = 128
BATCHES = 3
POS = 2


def extended(shard, sides, width):
    for axis, dim in sides:
        size, length = (lax.axis_size(axis), shard.shape[dim])
        up = [(i, (i + 1) % size) for i in range(size - 1)]
        down = [(j, i) for i, j in up]
        last = lax.slice_in_dim(shard, length - width, length, axis=dim)
        leading = lax.slice_in_dim(shard, 0, width, axis=dim)
        before = lax.ppermute(last, axis, up)
        after = lax.ppermute(leading, axis, down)
        shard = jnp.concatenate([before, shard, after], axis=dim)
    return shard


def shifted(value, axis, steps):
    count = lax.axis_size(axis)
    leading, last = (max(0, -steps), min(count, count - steps))
    return lax.ppermute(value, axis, [(source, source + steps) for source in range(leading, last)])


def dft_tables(size):
    index = jnp.arange(size, dtype=jnp.int32)
    phase = index[:, None] * index[None, :] % size
    angle = -2.0 * jnp.pi * phase.astype(jnp.float32) / size
    scale = 1.0 / jnp.sqrt(jnp.float32(size))
    return (jnp.cos(angle) * scale, jnp.sin(angle) * scale)


def transform(real_part, imag_part, table_re, table_im):
    high = lax.Precision.HIGHEST
    left_re = jnp.einsum("jk,mkl->mjl", table_re, real_part, precision=high) - jnp.einsum(
        "jk,mkl->mjl", table_im, imag_part, precision=high
    )
    left_im = jnp.einsum("jk,mkl->mjl", table_re, imag_part, precision=high) + jnp.einsum(
        "jk,mkl->mjl", table_im, real_part, precision=high
    )
    out_re = jnp.einsum("mjk,kl->mjl", left_re, table_re, precision=high) - jnp.einsum(
        "mjk,kl->mjl", left_im, table_im, precision=high
    )
    out_im = jnp.einsum("mjk,kl->mjl", left_re, table_im, precision=high) + jnp.einsum(
        "mjk,kl->mjl", left_im, table_re, precision=high
    )
    return (out_re, out_im)


def slot_terms(patch, probe, measured, table_re, table_im):
    probe_re = probe[:, 0]
    probe_im = probe[:, 1]
    obj_re = patch[0]
    obj_im = patch[1]
    psi_re = probe_re * obj_re - probe_im * obj_im
    psi_im = probe_re * obj_im + probe_im * obj_re
    far_re, far_im = transform(psi_re, psi_im, table_re, table_im)
    intensity = jnp.sum(far_re * far_re + far_im * far_im, axis=0)
    keep = 1.0 - jnp.sqrt(measured) / jnp.sqrt(intensity + 0.1)
    back_re, back_im = transform(far_re * keep, far_im * keep, table_re, -table_im)
    grad_re = jnp.sum(probe_re * back_re + probe_im * back_im, axis=0)
    grad_im = jnp.sum(probe_re * back_im - probe_im * back_re, axis=0)
    pgrad_re = obj_re * back_re + obj_im * back_im
    pgrad_im = obj_re * back_im - obj_im * back_re
    square = jnp.sum(obj_re * obj_re + obj_im * obj_im)
    return (jnp.stack([grad_re, grad_im]), jnp.stack([pgrad_re, pgrad_im], axis=1), square)


def local(object_field, probe, patterns, offsets, counts):
    tile = object_field.shape[1]
    size = probe.shape[-1]
    table_re, table_im = dft_tables(size)
    padded = extended(object_field, (("wide", 2), ("narrow", 1)), H)
    gradient = jnp.zeros_like(padded)
    count_here = counts[0, 0]
    zero_at = jnp.zeros((), jnp.int32)
    for minibatch in range(BATCHES):
        probe_grad = jnp.zeros_like(probe)
        coverage = jnp.zeros((), jnp.float32)
        for position in range(POS):
            slot_at = minibatch * POS + position
            row_at = offsets[0, 0, slot_at, 0] + H
            col_at = offsets[0, 0, slot_at, 1] + H
            patch = lax.dynamic_slice(padded, (zero_at, row_at, col_at), (2, size, size))
            measured = patterns[0, 0, slot_at]

            def active(operands):
                return slot_terms(operands[0], operands[1], operands[2], table_re, table_im)

            def inactive(operands):
                return (
                    jnp.zeros((2, size, size), jnp.float32),
                    jnp.zeros_like(probe),
                    jnp.zeros((), jnp.float32),
                )

            obj_grad, pgrad, square = lax.cond(
                slot_at < count_here, active, inactive, (patch, probe, measured)
            )
            old = lax.dynamic_slice(gradient, (zero_at, row_at, col_at), (2, size, size))
            gradient = lax.dynamic_update_slice(gradient, old + obj_grad, (zero_at, row_at, col_at))
            probe_grad = probe_grad + pgrad
            coverage = coverage + square
        summed, total_cover = lax.psum((probe_grad, coverage), ("wide", "narrow"))
        probe = probe - summed / (total_cover / (size * size))
    left_part = gradient[:, :, :H]
    right_part = gradient[:, :, tile + H :]
    from_right = shifted(left_part, "wide", -1)
    from_left = shifted(right_part, "wide", 1)
    gradient = gradient.at[:, :, tile : tile + H].add(from_right)
    gradient = gradient.at[:, :, H : 2 * H].add(from_left)
    upper_part = gradient[:, :H, H : tile + H]
    lower_part = gradient[:, tile + H :, H : tile + H]
    from_below = shifted(upper_part, "narrow", -1)
    from_above = shifted(lower_part, "narrow", 1)
    core = gradient[:, H : tile + H, H : tile + H]
    core = core.at[:, tile - H :, :].add(from_below)
    core = core.at[:, :H, :].add(from_above)
    power = jnp.sum(probe[:, 0] ** 2 + probe[:, 1] ** 2, axis=0)
    top = jnp.max(power)
    return (object_field - 0.5 * core / top, probe)


def solution(mesh):
    placed = (
        P(None, "narrow", "wide"),
        P(),
        P("narrow", "wide", None, None, None),
        P("narrow", "wide", None, None),
        P("narrow", "wide"),
    )
    return jax.shard_map(
        local,
        mesh=mesh,
        in_specs=placed,
        out_specs=(P(None, "narrow", "wide"), P()),
        check_vma=False,
    )
```

profile of v0, /device:TPU:1, one launch (start us, length us, event | category | flops | bytes accessed | tf_op | source)
XLA Modules:
  0.0 804.1 jit_solution(2545430750540542145)
XLA Ops:
  8.6 4.9 collective-permute-start
  15.5 4.2 collective-permute-done
  19.9 4.2 collective-permute-done.1
  27.1 3.2 collective-permute-start.2
  38.9 2.7 collective-permute-done.2
  41.6 4.1 collective-permute-done.3
  45.7 4.6 pad_maximum_fusion.12
  50.3 37.6 %conditional.6 = (f32[2,256,256]{2,1,0:T(8,128)S(1)}, f32[]{:T(128)}, f32[4,2,256,256]{3,2,1,0:T(8,128)}) conditional(s32[]{:T(128)} %bitcast.174, () %tuple.80, (f32[4,2,256,256]{3,2,1,0:T(8,128)S(1)}, f32[2,768,768]{2,1,0:T(8,128)}, f32[256,256]{1,0:T(8,128)S(1)}, f32[256,256]{1,0:T(8,128)S(1)}, f32[256,256]{1,0:T(8,128)S(1)}, ...), branch_computations={%region_0.1_spmd, %region_1.6_spmd.clone} | conditional | flops 12897091584 | bytes 71303224 | solution.py:102
  87.9 38.3 %conditional.7 = (f32[2,256,256]{2,1,0:T(8,128)S(1)}, f32[]{:T(128)}, f32[4,2,256,256]{3,2,1,0:T(8,128)}) conditional(s32[]{:T(128)} %bitcast.183, () %tuple.82, (f32[4,2,256,256]{3,2,1,0:T(8,128)S(1)}, f32[2,768,768]{2,1,0:T(8,128)}, f32[256,256]{1,0:T(8,128)S(1)}, f32[256,256]{1,0:T(8,128)S(1)}, f32[256,256]{1,0:T(8,128)S(1)}, ...), branch_computations={%region_6.7_spmd, %region_7.12_spmd.clone} | conditional | flops 12897091584 | bytes 71303224 | solution.py:102
  126.2 4.0 add.745
  135.5 71.5 %psum.43 = f32[]{:T(128)} all-reduce(f32[]{:T(128)S(6)} %add.746), channel_id=1, replica_groups=mesh['wide'=32,'narrow'=4] {'wide','narrow'}, use_global_device_ids=true, to_apply=%region_13.14 | all-reduce | flops 1 | bytes 8 | tf_op jit(solution)/shard_map/psum | solution.py:109
  207.7 80.3 %all-reduce.4.cloned.1.call-done = f32[4,2,256,256]{3,2,1,0:T(8,128)} async-done(((f32[4,2,256,256]{3,2,1,0:T(8,128)}), f32[4,2,256,256]{3,2,1,0:T(8,128)}) %all-reduce.4.cloned.1.call-update) | async-done | bytes 2097168 | tf_op jit(solution)/shard_map/psum | solution.py:109
  288.1 2.6 divide_subtract_fusion.3
  290.6 37.3 %conditional.8 = (f32[2,256,256]{2,1,0:T(8,128)}, f32[]{:T(128)}, f32[4,2,256,256]{3,2,1,0:T(8,128)}) conditional(s32[]{:T(128)} %bitcast.188, () %tuple.84, (f32[4,2,256,256]{3,2,1,0:T(8,128)S(1)}, f32[2,768,768]{2,1,0:T(8,128)}, s32[]{:T(128)}, s32[]{:T(128)}, f32[256,256]{1,0:T(8,128)S(1)}, /*index=5*/f32[256,256]{1,0:T(8,128)S(1)}, ...), branch_computations={%region_14.15_spmd, %region_15.20_spmd} | conditional | flops 12897091584 | bytes 71303224 | solution.py:102
  327.9 12.4 %conditional.9 = (f32[2,256,256]{2,1,0:T(8,128)}, f32[]{:T(128)}, f32[4,2,256,256]{3,2,1,0:T(8,128)}) conditional(s32[]{:T(128)} %bitcast.193, () %tuple.86, (f32[4,2,256,256]{3,2,1,0:T(8,128)S(1)}, f32[2,768,768]{2,1,0:T(8,128)}, s32[]{:T(128)}, s32[]{:T(128)}, f32[256,256]{1,0:T(8,128)S(1)}, /*index=5*/f32[256,256]{1,0:T(8,128)S(1)}, ...), branch_computations={%region_20.21_spmd, %region_21.26_spmd} | conditional | flops 12897091584 | bytes 71303224 | solution.py:102
  340.3 3.8 add.765
  351.4 6.5 dynamic_update_slice.18
  359.4 6.6 dynamic_update_slice.19
  366.1 89.8 %psum.45 = f32[]{:T(128)} all-reduce(f32[]{:T(128)S(6)} %add.766), channel_id=1, replica_groups=mesh['wide'=32,'narrow'=4] {'wide','narrow'}, use_global_device_ids=true, to_apply=%region_27.28 | all-reduce | flops 1 | bytes 8 | tf_op jit(solution)/shard_map/psum | solution.py:109
  458.1 6.4 dynamic_update_slice.20
  466.0 6.6 dynamic_update_slice.21
  472.6 45.5 %all-reduce.6.cloned.1.call-done = f32[4,2,256,256]{3,2,1,0:T(8,128)} async-done(((f32[4,2,256,256]{3,2,1,0:T(8,128)}), f32[4,2,256,256]{3,2,1,0:T(8,128)}) %all-reduce.6.cloned.1.call-update) | async-done | bytes 2097168 | tf_op jit(solution)/shard_map/psum | solution.py:109
  518.1 3.2 divide_subtract_fusion.2
  521.3 11.7 %conditional.10 = (f32[2,256,256]{2,1,0:T(8,128)}, f32[]{:T(128)}, f32[4,2,256,256]{3,2,1,0:T(8,128)}) conditional(s32[]{:T(128)} %bitcast.198, () %tuple.88, (f32[4,2,256,256]{3,2,1,0:T(8,128)}, f32[2,768,768]{2,1,0:T(8,128)}, s32[]{:T(128)}, s32[]{:T(128)}, f32[256,256]{1,0:T(8,128)S(1)}, /*index=5*/f32[256,256]{1,0:T(8,128)S(1)}, ...), branch_computations={%region_28.29_spmd, %region_29.34_spmd} | conditional | flops 12897091584 | bytes 79691856 | solution.py:102
  534.6 6.8 dynamic_update_slice.22
  541.4 5.4 conditional.11
  548.2 6.9 dynamic_update_slice.23
  556.3 60.8 %collective-permute-start.4 = (f32[2,768,128]{2,1,0:T(8,128)S(1)}, f32[2,768,128]{2,1,0:T(8,128)S(1)}, u32[]{:S(2)}, u32[]{:S(2)}) collective-permute-start(f32[2,768,128]{2,1,0:T(8,128)S(1)} %slice.336), channel_id=1, source_target_pairs={{4,0},{8,4},{12,8},{16,12},{20,16},{24,20},{28,24},{32,28},{36,32}... | collective-permute-start | bytes 2359304 | tf_op jit(solution)/shard_map/ppermute | solution.py:27
  619.0 2.7 fusion.259
  623.7 3.8 add.781
  627.5 75.8 %psum.47 = f32[]{:T(128)} all-reduce(f32[]{:T(128)S(6)} %add.782), channel_id=1, replica_groups=mesh['wide'=32,'narrow'=4] {'wide','narrow'}, use_global_device_ids=true, to_apply=%region_41.42 | all-reduce | flops 1 | bytes 8 | tf_op jit(solution)/shard_map/psum | solution.py:109
  711.0 76.2 %all-reduce.8.cloned.1.call-done = f32[4,2,256,256]{3,2,1,0:T(8,128)} async-done(((f32[4,2,256,256]{3,2,1,0:T(8,128)}), f32[4,2,256,256]{3,2,1,0:T(8,128)}) %all-reduce.8.cloned.1.call-update) | async-done | bytes 2097168 | tf_op jit(solution)/shard_map/psum | solution.py:109
  (123 shorter events, 154.6 us)
Async XLA Ops:
  7.2 12.6 %copy-start.3 = (f32[2,512,512]{2,1,0:T(8,128)S(1)}, f32[2,512,512]{2,1,0:T(8,128)}, u32[]{:S(2)}) copy-start(f32[2,512,512]{2,1,0:T(8,128)} %param.25) | copy-start | bytes 6291460
  7.2 280.9 %all-reduce.4.cloned.1.call-start = ((), (), s32[]{:S(2)}) async-start(), calls=%async_computation | async-start | bytes 4194304 | tf_op jit(solution)/shard_map/psum | solution.py:109
  8.6 11.0 %collective-permute-start = (f32[2,512,128]{2,1,0:T(8,128)S(1)}, f32[2,512,128]{2,1,0:T(8,128)S(1)}, u32[]{:S(2)}, u32[]{:S(2)}) collective-permute-start(f32[2,512,128]{2,1,0:T(8,128)S(1)} %get-tuple-element.871), channel_id=1, source_target_pairs={{0,4},{4,8},{8,12},{12,16},{16,20},{20,24},{24,28},{28,32},{32,36}... | collective-permute-start | bytes 1572872 | tf_op jit(solution)/shard_map/ppermute | solution.py:18
  13.6 10.5 %collective-permute-start.1 = (f32[2,512,128]{2,1,0:T(8,128)S(1)}, f32[2,512,128]{2,1,0:T(8,128)S(1)}, u32[]{:S(2)}, u32[]{:S(2)}) collective-permute-start(f32[2,512,128]{2,1,0:T(8,128)S(1)} %get-tuple-element.870), channel_id=1, source_target_pairs={{4,0},{8,4},{12,8},{16,12},{20,16},{24,20},{28,24},{32,28},{36,32}... | collective-permute-start | bytes 1572872 | tf_op jit(solution)/shard_map/ppermute | solution.py:19
  19.9 11.6 %copy-start.8 = (s32[1,1,6,2]{2,3,1,0:T(2,128)S(1)}, s32[1,1,6,2]{2,3,1,0:T(2,128)}, u32[]{:S(2)}) copy-start(s32[1,1,6,2]{2,3,1,0:T(2,128)} %param.28) | copy-start | bytes 148
  24.1 1.7 copy-start.5
  27.1 14.5 %collective-permute-start.2 = (f32[2,128,768]{2,1,0:T(8,128)}, f32[2,128,768]{2,1,0:T(8,128)S(1)}, u32[]{:S(2)}, u32[]{:S(2)}) collective-permute-start(f32[2,128,768]{2,1,0:T(8,128)} %get-tuple-element.868), channel_id=1, source_target_pairs={{0,1},{1,2},{2,3},{4,5},{5,6},{6,7},{8,9},{9,10},{10,11},{12,13},{... | collective-permute-start | bytes 2359304 | tf_op jit(solution)/shard_map/ppermute | solution.py:18
  30.2 15.5 %collective-permute-start.3 = (f32[2,128,768]{2,1,0:T(8,128)}, f32[2,128,768]{2,1,0:T(8,128)}, u32[]{:S(2)}, u32[]{:S(2)}) collective-permute-start(f32[2,128,768]{2,1,0:T(8,128)} %get-tuple-element.869), channel_id=1, source_target_pairs={{1,0},{2,1},{3,2},{5,4},{6,5},{7,6},{9,8},{10,9},{11,10},{13,12},{... | collective-permute-start | bytes 2359304 | tf_op jit(solution)/shard_map/ppermute | solution.py:19
  38.9 11.4 %copy-start.2 = (f32[4,2,256,256]{3,2,1,0:T(8,128)S(1)}, f32[4,2,256,256]{3,2,1,0:T(8,128)}, u32[]{:S(2)}) copy-start(f32[4,2,256,256]{3,2,1,0:T(8,128)} %param.26) | copy-start | bytes 6291460
  126.2 4.0 copy-start.7
  130.3 387.8 %all-reduce.6.cloned.1.call-start = ((), (), s32[]{:S(2)}) async-start(), calls=%async_computation.1 | async-start | bytes 4194304 | tf_op jit(solution)/shard_map/psum | solution.py:109
  344.1 443.1 %all-reduce.8.cloned.1.call-start = ((), (), s32[]{:S(2)}) async-start(), calls=%async_computation.2 | async-start | bytes 4194304 | tf_op jit(solution)/shard_map/psum | solution.py:109
  532.9 8.5 %copy-start = (f32[4,2,256,256]{3,2,1,0:T(8,128)S(1)}, f32[4,2,256,256]{3,2,1,0:T(8,128)}, u32[]{:S(2)}) copy-start(f32[4,2,256,256]{3,2,1,0:T(8,128)} %divide_subtract_fusion.2) | copy-start | bytes 6291460
  556.3 62.7 %collective-permute-start.4 = (f32[2,768,128]{2,1,0:T(8,128)S(1)}, f32[2,768,128]{2,1,0:T(8,128)S(1)}, u32[]{:S(2)}, u32[]{:S(2)}) collective-permute-start(f32[2,768,128]{2,1,0:T(8,128)S(1)} %slice.336), channel_id=1, source_target_pairs={{4,0},{8,4},{12,8},{16,12},{20,16},{24,20},{28,24},{32,28},{36,32}... | collective-permute-start | bytes 2359304 | tf_op jit(solution)/shard_map/ppermute | solution.py:27
  621.8 82.2 %collective-permute-start.5 = (f32[2,768,128]{2,1,0:T(8,128)}, f32[2,768,128]{2,1,0:T(8,128)S(1)}, u32[]{:S(2)}, u32[]{:S(2)}) collective-permute-start(f32[2,768,128]{2,1,0:T(8,128)} %get-tuple-element.866), channel_id=1, source_target_pairs={{0,4},{4,8},{8,12},{12,16},{16,20},{20,24},{24,28},{28,32},{32,36}... | collective-permute-start | bytes 2359304 | tf_op jit(solution)/shard_map/ppermute | solution.py:27
  708.4 86.1 %collective-permute-start.7 = (f32[2,128,512]{2,1,0:T(8,128)}, f32[2,128,512]{2,1,0:T(8,128)S(1)}, u32[]{:S(2)}, u32[]{:S(2)}) collective-permute-start(f32[2,128,512]{2,1,0:T(8,128)} %get-tuple-element.864), channel_id=1, source_target_pairs={{0,1},{1,2},{2,3},{4,5},{5,6},{6,7},{8,9},{9,10},{10,11},{12,13},{... | collective-permute-start | bytes 1572872 | tf_op jit(solution)/shard_map/ppermute | solution.py:27
  709.7 83.3 %collective-permute-start.6 = (f32[2,128,512]{2,1,0:T(8,128)}, f32[2,128,512]{2,1,0:T(8,128)}, u32[]{:S(2)}, u32[]{:S(2)}) collective-permute-start(f32[2,128,512]{2,1,0:T(8,128)} %get-tuple-element.865), channel_id=1, source_target_pairs={{1,0},{2,1},{3,2},{5,4},{6,5},{7,6},{9,8},{10,9},{11,10},{13,12},{... | collective-permute-start | bytes 1572872 | tf_op jit(solution)/shard_map/ppermute | solution.py:27
  789.1 1.3 copy-start.6
  793.0 1.9 copy-start.4
Sparse Core Ops, SparseCore 0:
  130.4 157.6 all-reduce.3
  344.3 173.7 all-reduce.5
  627.6 159.5 all-reduce.7
where the time goes:
time: 809 us; the launch traced here: 804 us
  blocking collectives  237 us (29%)
  waiting for transfers between devices  219 us (27%)
  matrix products  91.7 us (11%)
  starting transfers between devices  76.8 us (9%)
  local copies, waits for them, and re-layouts  65 us (8%)
  other arithmetic  52.5 us (6%)
  between operations  31.9 us (4%)
  loops' own time  29.9 us (4%)
    psum x3, blocking collectives, local(): summed, total_cover = lax.psum((probe_grad, coverage), ('wide', 'narrow'))  237 us
    psum x3, waiting for transfers between devices, local(): summed, total_cover = lax.psum((probe_grad, coverage), ('wide', 'narrow'))  202 us
    ppermute x4, starting transfers between devices, shifted(): lax.ppermute(value, axis, [(source, source + steps) for source in range(l...  65.4 us
    dynamic_update_slice x6, local copies, waits for them, and re-layouts, local(): lax.dynamic_update_slice(gradient, old + obj_grad, (zero_at, row_at, col_...  39.8 us
    another operation x6, loops' own time, local(): lax.cond(slot_at < count_here, active, inactive, (patch, probe, measured))  29.9 us
  transfers between devices with their start and end apart: 11, of which 8 were waited for; matrix products, arithmetic and copies ran while one was open for 6% of the time, Pallas kernels for 0%

commit v1 on v0

--- a/solution.py
+++ b/solution.py
@@ -106,7 +106,7 @@
             gradient = lax.dynamic_update_slice(gradient, old + obj_grad, (zero_at, row_at, col_at))
             probe_grad = probe_grad + pgrad
             coverage = coverage + square
-        summed, total_cover = lax.psum((probe_grad, coverage), ("wide", "narrow"))
+        summed, total_cover = lax.psum(lax.psum((probe_grad, coverage), "narrow"), "wide")
         probe = probe - summed / (total_cover / (size * size))
     left_part = gradient[:, :, :H]
     right_part = gradient[:, :, tile + H :]

time: 809 us -> 851 us (1.052)
  waiting for transfers between devices: 219 us -> 264 us
  blocking collectives: 237 us -> 226 us
    psum x3 -> x6, waiting for transfers between devices: 202 us -> 240 us  [the longest x3 186 us: local(): lax.psum((probe_grad, coverage), 'narrow')]
    psum x3 -> x6, blocking collectives: 237 us -> 226 us  [the longest x3 196 us: local(): lax.psum(lax.psum((probe_grad, coverage), 'narrow'), 'wide')]
  transfers between devices with their start and end apart: 11 -> 14, of which waited for: 8 -> 10; matrix products, arithmetic and copies ran while one was open for 6% -> 6% of each run, Pallas kernels for 0% -> 0%
where the time goes in v1:
time: 851 us; the launch traced here: 846 us
  waiting for transfers between devices  264 us (31%)
  blocking collectives  226 us (27%)
  matrix products  91.7 us (11%)
  starting transfers between devices  81.1 us (10%)
  local copies, waits for them, and re-layouts  66.7 us (8%)
  other arithmetic  57.2 us (7%)
  between operations  32 us (4%)
  loops' own time  27.4 us (3%)
    psum x3, blocking collectives, local(): lax.psum(lax.psum((probe_grad, coverage), 'narrow'), 'wide')  196 us
    psum x3, waiting for transfers between devices, local(): lax.psum((probe_grad, coverage), 'narrow')  186 us
    ppermute x4, starting transfers between devices, shifted(): lax.ppermute(value, axis, [(source, source + steps) for source in range(l...  69.6 us
    psum x3, waiting for transfers between devices, local(): lax.psum(lax.psum((probe_grad, coverage), 'narrow'), 'wide')  53.8 us
    dynamic_update_slice x6, local copies, waits for them, and re-layouts, local(): lax.dynamic_update_slice(gradient, old + obj_grad, (zero_at, row_at, col_...  39.8 us
    psum x3, blocking collectives, local(): lax.psum((probe_grad, coverage), 'narrow')  29.8 us
    another operation x6, loops' own time, local(): lax.cond(slot_at < count_here, active, inactive, (patch, probe, measured))  27.4 us
  transfers between devices with their start and end apart: 14, of which 10 were waited for; matrix products, arithmetic and copies ran while one was open for 6% of the time, Pallas kernels for 0%

profile of v1, /device:TPU:1, one launch (start us, length us, event | category | flops | bytes accessed | tf_op | source)
XLA Modules:
  0.0 846.1 jit_solution(9849578071049200219)
XLA Ops:
  8.6 4.9 collective-permute-start
  15.5 4.2 collective-permute-done
  19.9 4.2 collective-permute-done.1
  41.6 4.1 collective-permute-done.3
  45.7 4.6 pad_maximum_fusion.12
  50.3 37.7 %conditional.6 = (f32[2,256,256]{2,1,0:T(8,128)S(1)}, f32[]{:T(128)}, f32[4,2,256,256]{3,2,1,0:T(8,128)}) conditional(s32[]{:T(128)} %bitcast.174, () %tuple.80, (f32[4,2,256,256]{3,2,1,0:T(8,128)S(1)}, f32[2,768,768]{2,1,0:T(8,128)}, f32[256,256]{1,0:T(8,128)S(1)}, f32[256,256]{1,0:T(8,128)S(1)}, f32[256,256]{1,0:T(8,128)S(1)}, ...), branch_computations={%region_0.1_spmd, %region_1.6_spmd.clone} | conditional | flops 12897091584 | bytes 71303224 | solution.py:102
  88.0 37.8 %conditional.7 = (f32[2,256,256]{2,1,0:T(8,128)}, f32[]{:T(128)}, f32[4,2,256,256]{3,2,1,0:T(8,128)}) conditional(s32[]{:T(128)} %bitcast.183, () %tuple.82, (f32[4,2,256,256]{3,2,1,0:T(8,128)S(1)}, f32[2,768,768]{2,1,0:T(8,128)}, f32[256,256]{1,0:T(8,128)S(1)}, f32[256,256]{1,0:T(8,128)S(1)}, f32[256,256]{1,0:T(8,128)S(1)}, ...), branch_computations={%region_6.7_spmd, %region_7.12_spmd.clone} | conditional | flops 12897091584 | bytes 71303224 | solution.py:102
  125.8 3.8 add.757
  129.7 65.1 %all-reduce.7.cloned.1.call-done = f32[4,2,256,256]{3,2,1,0:T(8,128)} async-done(((f32[4,2,256,256]{3,2,1,0:T(8,128)}), f32[4,2,256,256]{3,2,1,0:T(8,128)}) %all-reduce.7.cloned.1.call-update) | async-done | bytes 2097168 | tf_op jit(solution)/shard_map/psum | solution.py:109
  199.7 7.1 psum.86
  206.8 65.8 %psum.87 = f32[]{:T(128)} all-reduce(f32[]{:T(128)} %psum.86), channel_id=1, replica_groups=mesh['wide'=32,'narrow'=4] {'wide'}, use_global_device_ids=true, to_apply=%region_15.16 | all-reduce | flops 1 | bytes 8 | tf_op jit(solution)/shard_map/psum | solution.py:109
  273.2 32.6 %all-reduce.9.cloned.1.call-done = f32[4,2,256,256]{3,2,1,0:T(8,128)} async-done(((f32[4,2,256,256]{3,2,1,0:T(8,128)}), f32[4,2,256,256]{3,2,1,0:T(8,128)}) %all-reduce.9.cloned.1.call-update) | async-done | bytes 2097168 | tf_op jit(solution)/shard_map/psum | solution.py:109
  308.4 37.1 %conditional.8 = (f32[2,256,256]{2,1,0:T(8,128)}, f32[]{:T(128)}, f32[4,2,256,256]{3,2,1,0:T(8,128)}) conditional(s32[]{:T(128)} %bitcast.188, () %tuple.84, (f32[4,2,256,256]{3,2,1,0:T(8,128)S(1)}, f32[2,768,768]{2,1,0:T(8,128)}, s32[]{:T(128)}, s32[]{:T(128)}, f32[256,256]{1,0:T(8,128)S(1)}, /*index=5*/f32[256,256]{1,0:T(8,128)S(1)}, ...), branch_computations={%region_16.17_spmd, %region_17.22_spmd} | conditional | flops 12897091584 | bytes 71303224 | solution.py:102
  345.6 11.8 %conditional.9 = (f32[2,256,256]{2,1,0:T(8,128)}, f32[]{:T(128)}, f32[4,2,256,256]{3,2,1,0:T(8,128)}) conditional(s32[]{:T(128)} %bitcast.193, () %tuple.86, (f32[4,2,256,256]{3,2,1,0:T(8,128)S(1)}, f32[2,768,768]{2,1,0:T(8,128)}, s32[]{:T(128)}, s32[]{:T(128)}, f32[256,256]{1,0:T(8,128)S(1)}, /*index=5*/f32[256,256]{1,0:T(8,128)S(1)}, ...), branch_computations={%region_22.23_spmd, %region_23.28_spmd} | conditional | flops 12897091584 | bytes 71303224 | solution.py:102
  361.3 83.4 %all-reduce.11.cloned.1.call-done = f32[4,2,256,256]{3,2,1,0:T(8,128)} async-done(((f32[4,2,256,256]{3,2,1,0:T(8,128)}), f32[4,2,256,256]{3,2,1,0:T(8,128)}) %all-reduce.11.cloned.1.call-update) | async-done | bytes 2097168 | tf_op jit(solution)/shard_map/psum | solution.py:109
  452.2 6.5 dynamic_update_slice.18
  460.2 7.8 psum.90
  468.0 6.6 dynamic_update_slice.19
  474.6 64.8 %psum.91 = f32[]{:T(128)} all-reduce(f32[]{:T(128)} %psum.90), channel_id=1, replica_groups=mesh['wide'=32,'narrow'=4] {'wide'}, use_global_device_ids=true, to_apply=%region_31.32 | all-reduce | flops 1 | bytes 8 | tf_op jit(solution)/shard_map/psum | solution.py:109
  541.6 6.4 dynamic_update_slice.20
  549.6 6.6 dynamic_update_slice.21
  559.3 11.7 %conditional.10 = (f32[2,256,256]{2,1,0:T(8,128)}, f32[]{:T(128)}, f32[4,2,256,256]{3,2,1,0:T(8,128)}) conditional(s32[]{:T(128)} %bitcast.198, () %tuple.88, (f32[4,2,256,256]{3,2,1,0:T(8,128)}, f32[2,768,768]{2,1,0:T(8,128)}, s32[]{:T(128)}, s32[]{:T(128)}, f32[256,256]{1,0:T(8,128)S(1)}, /*index=5*/f32[256,256]{1,0:T(8,128)S(1)}, ...), branch_computations={%region_32.33_spmd, %region_33.38_spmd} | conditional | flops 12897091584 | bytes 79691856 | solution.py:102
  572.6 6.8 dynamic_update_slice.22
  579.4 4.8 conditional.11
  585.7 6.9 dynamic_update_slice.23
  593.7 64.5 %collective-permute-start.4 = (f32[2,768,128]{2,1,0:T(8,128)S(1)}, f32[2,768,128]{2,1,0:T(8,128)}, u32[]{:S(2)}, u32[]{:S(2)}) collective-permute-start(f32[2,768,128]{2,1,0:T(8,128)S(1)} %slice.336), channel_id=1, source_target_pairs={{4,0},{8,4},{12,8},{16,12},{20,16},{24,20},{28,24},{32,28},{36,32}... | collective-permute-start | bytes 2359304 | tf_op jit(solution)/shard_map/ppermute | solution.py:27
  666.7 8.9 %collective-permute-done.5 = f32[2,768,128]{2,1,0:T(8,128)S(1)} collective-permute-done((f32[2,768,128]{2,1,0:T(8,128)S(1)}, f32[2,768,128]{2,1,0:T(8,128)S(1)}, u32[]{:S(2)}, u32[]{:S(2)}) %collective-permute-start.5) | collective-permute-done | bytes 786464 | tf_op jit(solution)/shard_map/ppermute | solution.py:27
  681.4 37.6 %all-reduce.15.cloned.1.call-done = f32[4,2,256,256]{3,2,1,0:T(8,128)} async-done(((f32[4,2,256,256]{3,2,1,0:T(8,128)}), f32[4,2,256,256]{3,2,1,0:T(8,128)}) %all-reduce.15.cloned.1.call-update) | async-done | bytes 2097168 | tf_op jit(solution)/shard_map/psum | solution.py:109
  721.0 14.9 %psum.94 = f32[]{:T(128)} all-reduce(f32[]{:T(128)S(6)} %add.794), channel_id=1, replica_groups=mesh['wide'=32,'narrow'=4] {'narrow'}, use_global_device_ids=true, to_apply=%region_46.47 | all-reduce | flops 1 | bytes 8 | tf_op jit(solution)/shard_map/psum | solution.py:109
  735.9 65.4 %psum.95 = f32[]{:T(128)} all-reduce(f32[]{:T(128)} %psum.94), channel_id=1, replica_groups=mesh['wide'=32,'narrow'=4] {'wide'}, use_global_device_ids=true, to_apply=%region_47.48 | all-reduce | flops 1 | bytes 8 | tf_op jit(solution)/shard_map/psum | solution.py:109
  809.0 21.2 %all-reduce.17.cloned.1.call-done = f32[4,2,256,256]{3,2,1,0:T(8,128)} async-done(((f32[4,2,256,256]{3,2,1,0:T(8,128)}), f32[4,2,256,256]{3,2,1,0:T(8,128)}) %all-reduce.17.cloned.1.call-update) | async-done | bytes 2097168 | tf_op jit(solution)/shard_map/psum | solution.py:109
  834.9 4.1 divide_subtract_fusion
  (133 shorter events, 178.1 us)
Async XLA Ops:
  7.2 12.6 %copy-start.3 = (f32[2,512,512]{2,1,0:T(8,128)S(1)}, f32[2,512,512]{2,1,0:T(8,128)}, u32[]{:S(2)}) copy-start(f32[2,512,512]{2,1,0:T(8,128)} %param.25) | copy-start | bytes 6291460
  7.2 187.6 %all-reduce.7.cloned.1.call-start = ((), (), s32[]{:S(2)}) async-start(), calls=%async_computation | async-start | bytes 4194304 | tf_op jit(solution)/shard_map/psum | solution.py:109
  8.6 11.0 %collective-permute-start = (f32[2,512,128]{2,1,0:T(8,128)S(1)}, f32[2,512,128]{2,1,0:T(8,128)S(1)}, u32[]{:S(2)}, u32[]{:S(2)}) collective-permute-start(f32[2,512,128]{2,1,0:T(8,128)S(1)} %get-tuple-element.871), channel_id=1, source_target_pairs={{0,4},{4,8},{8,12},{12,16},{16,20},{20,24},{24,28},{28,32},{32,36}... | collective-permute-start | bytes 1572872 | tf_op jit(solution)/shard_map/ppermute | solution.py:18
  13.6 10.5 %collective-permute-start.1 = (f32[2,512,128]{2,1,0:T(8,128)S(1)}, f32[2,512,128]{2,1,0:T(8,128)S(1)}, u32[]{:S(2)}, u32[]{:S(2)}) collective-permute-start(f32[2,512,128]{2,1,0:T(8,128)S(1)} %get-tuple-element.870), channel_id=1, source_target_pairs={{4,0},{8,4},{12,8},{16,12},{20,16},{24,20},{28,24},{32,28},{36,32}... | collective-permute-start | bytes 1572872 | tf_op jit(solution)/shard_map/ppermute | solution.py:19
  19.9 11.6 %copy-start.7 = (s32[1,1,6,2]{2,3,1,0:T(2,128)S(1)}, s32[1,1,6,2]{2,3,1,0:T(2,128)}, u32[]{:S(2)}) copy-start(s32[1,1,6,2]{2,3,1,0:T(2,128)} %param.28) | copy-start | bytes 148
  24.1 1.7 copy-start.5
  27.1 14.5 %collective-permute-start.2 = (f32[2,128,768]{2,1,0:T(8,128)}, f32[2,128,768]{2,1,0:T(8,128)S(1)}, u32[]{:S(2)}, u32[]{:S(2)}) collective-permute-start(f32[2,128,768]{2,1,0:T(8,128)} %get-tuple-element.868), channel_id=1, source_target_pairs={{0,1},{1,2},{2,3},{4,5},{5,6},{6,7},{8,9},{9,10},{10,11},{12,13},{... | collective-permute-start | bytes 2359304 | tf_op jit(solution)/shard_map/ppermute | solution.py:18
  30.2 15.5 %collective-permute-start.3 = (f32[2,128,768]{2,1,0:T(8,128)}, f32[2,128,768]{2,1,0:T(8,128)}, u32[]{:S(2)}, u32[]{:S(2)}) collective-permute-start(f32[2,128,768]{2,1,0:T(8,128)} %get-tuple-element.869), channel_id=1, source_target_pairs={{1,0},{2,1},{3,2},{5,4},{6,5},{7,6},{9,8},{10,9},{11,10},{13,12},{... | collective-permute-start | bytes 2359304 | tf_op jit(solution)/shard_map/ppermute | solution.py:19
  38.8 11.5 %copy-start.2 = (f32[4,2,256,256]{3,2,1,0:T(8,128)S(1)}, f32[4,2,256,256]{3,2,1,0:T(8,128)}, u32[]{:S(2)}) copy-start(f32[4,2,256,256]{3,2,1,0:T(8,128)} %param.26) | copy-start | bytes 6291460
  129.6 176.2 %all-reduce.9.cloned.1.call-start = ((), (), s32[]{:S(2)}) async-start(), calls=%async_computation.1 | async-start | bytes 4194304 | tf_op jit(solution)/shard_map/psum | solution.py:109
  194.8 249.9 %all-reduce.11.cloned.1.call-start = ((), (), s32[]{:S(2)}) async-start(), calls=%async_computation.2 | async-start | bytes 4194304 | tf_op jit(solution)/shard_map/psum | solution.py:109
  361.2 194.9 %all-reduce.13.cloned.1.call-start = ((), (), s32[]{:S(2)}) async-start(), calls=%async_computation.3 | async-start | bytes 4194304 | tf_op jit(solution)/shard_map/psum | solution.py:109
  444.7 274.3 %all-reduce.15.cloned.1.call-start = ((), (), s32[]{:S(2)}) async-start(), calls=%async_computation.4 | async-start | bytes 4194304 | tf_op jit(solution)/shard_map/psum | solution.py:109
  571.0 8.5 %copy-start = (f32[4,2,256,256]{3,2,1,0:T(8,128)S(1)}, f32[4,2,256,256]{3,2,1,0:T(8,128)}, u32[]{:S(2)}) copy-start(f32[4,2,256,256]{3,2,1,0:T(8,128)} %divide_subtract_fusion.2) | copy-start | bytes 6291460
  593.7 68.4 %collective-permute-start.4 = (f32[2,768,128]{2,1,0:T(8,128)S(1)}, f32[2,768,128]{2,1,0:T(8,128)}, u32[]{:S(2)}, u32[]{:S(2)}) collective-permute-start(f32[2,768,128]{2,1,0:T(8,128)S(1)} %slice.336), channel_id=1, source_target_pairs={{4,0},{8,4},{12,8},{16,12},{20,16},{24,20},{28,24},{32,28},{36,32}... | collective-permute-start | bytes 2359304 | tf_op jit(solution)/shard_map/ppermute | solution.py:27
  662.0 168.1 %all-reduce.17.cloned.1.call-start = ((), (), s32[]{:S(2)}) async-start(), calls=%async_computation.5 | async-start | bytes 4194304 | tf_op jit(solution)/shard_map/psum | solution.py:109
  664.8 10.8 %collective-permute-start.5 = (f32[2,768,128]{2,1,0:T(8,128)S(1)}, f32[2,768,128]{2,1,0:T(8,128)S(1)}, u32[]{:S(2)}, u32[]{:S(2)}) collective-permute-start(f32[2,768,128]{2,1,0:T(8,128)S(1)} %get-tuple-element.866), channel_id=1, source_target_pairs={{0,4},{4,8},{8,12},{12,16},{16,20},{20,24},{24,28},{28,32},{32,36}... | collective-permute-start | bytes 2359304 | tf_op jit(solution)/shard_map/ppermute | solution.py:27
  680.1 125.0 %collective-permute-start.6 = (f32[2,128,512]{2,1,0:T(8,128)}, f32[2,128,512]{2,1,0:T(8,128)S(1)}, u32[]{:S(2)}, u32[]{:S(2)}) collective-permute-start(f32[2,128,512]{2,1,0:T(8,128)} %get-tuple-element.865), channel_id=1, source_target_pairs={{1,0},{2,1},{3,2},{5,4},{6,5},{7,6},{9,8},{10,9},{11,10},{13,12},{... | collective-permute-start | bytes 1572872 | tf_op jit(solution)/shard_map/ppermute | solution.py:27
  719.0 88.0 %collective-permute-start.7 = (f32[2,128,512]{2,1,0:T(8,128)}, f32[2,128,512]{2,1,0:T(8,128)S(1)}, u32[]{:S(2)}, u32[]{:S(2)}) collective-permute-start(f32[2,128,512]{2,1,0:T(8,128)} %get-tuple-element.864), channel_id=1, source_target_pairs={{0,1},{1,2},{2,3},{4,5},{5,6},{6,7},{8,9},{9,10},{10,11},{12,13},{... | collective-permute-start | bytes 1572872 | tf_op jit(solution)/shard_map/ppermute | solution.py:27
  832.0 1.3 copy-start.6
  833.3 1.6 copy-start.4
Sparse Core Ops, SparseCore 0:
  129.7 64.9 all-reduce.6
  198.0 107.7 all-reduce.8
  361.3 83.2 all-reduce.10
  447.8 107.8 all-reduce.12
  662.1 56.8 all-reduce.14
  722.1 107.9 all-reduce.16
